TPU v7x, 32 devices: a whole 2x2x4 slice. The times are simulated.
32 devices in a mesh: parts: 2 (over y), tok: 4 (over z), hid: 4 (over x, core).
Axes of the slice: x: 2, y: 2, z: 4, core: 2. Of those that a mesh axis runs over, the one named last changes fastest.
Arguments:
- tokens: bfloat16 [6144, 8192], P(('parts', 'tok'), 'hid'), parts along dimension 0, may hold values from -6 to 6
- adapter_ids: int32 [6144, 1], P(('parts', 'tok')), parts along dimension 0, may hold values from 0 to 31; in each aligned block of 768 rows (0 to 767, 768 to 1535, ...) at most 72 rows name the same one
- value_weight: bfloat16 [8192, 1024], P('hid'), may hold values from -0.0625 to 0.0625
- adapter_down: bfloat16 [32, 16, 8192], P('tok', None, 'hid'), may hold values from -0.0625 to 0.0625
- adapter_up: bfloat16 [32, 16, 1024], P('tok', None, 'hid'), may hold values from -1.5 to 1.5
Outputs:
- value_out: bfloat16 [6144, 1024], P(('parts', 'tok'), 'hid'), parts along dimension 0
There are 2 independent parts, one for each index of `parts`. A program takes and returns all parts, laid end to end along the dimension named above; an argument that names none is the same for every part. Nothing has to cross between parts.
Inputs may be any that keep to these rules, and one draw needn't show every extreme that they name: `adapter_ids`: among the 768 tokens of one index of tok, each adapter id appears at most 72 times; in some of these aligned blocks one id appears exactly 72 times.
All inputs are finite; a program needn't handle non-finite values.
Results may differ from a plain program's by a relative error of at most 0.0048.
Values may be sent and summed in bfloat16 or wider, within the bound.
A program may use at most 128 MiB of HBM per device.

v0:
```python
import jax
import jax.numpy as jnp
from jax import lax
from jax.sharding import PartitionSpec as P


def per_device(tokens, adapter_ids, value_weight, adapter_down, adapter_up):
    tok_rows, d_local = tokens.shape
    n_tok = lax.axis_size("tok")
    adp_dev = adapter_down.shape[0]
    low_rank = adapter_down.shape[1]
    kv_local = adapter_up.shape[2]
    adapters_all = adp_dev * n_tok
    capacity = max(2, 3 * tok_rows // adapters_all)
    token_ids = adapter_ids[:, 0]
    matches = token_ids[:, None] == token_ids[None, :]
    before = lax.broadcasted_iota(jnp.int32, (tok_rows, tok_rows), 0) > lax.broadcasted_iota(
        jnp.int32, (tok_rows, tok_rows), 1
    )
    position = jnp.sum((matches & before).astype(jnp.int32), axis=1)
    slot_index = token_ids * capacity + position
    slot_rows = (
        jnp.zeros((adapters_all * capacity, d_local), jnp.bfloat16).at[slot_index].set(tokens)
    )
    base_sums = lax.psum_scatter(
        lax.dot_general(
            value_weight, tokens, (((0,), (1,)), ((), ())), preferred_element_type=jnp.float32
        ),
        "hid",
        scatter_dimension=0,
        tiled=True,
    )
    weights_piece = lax.all_gather(adapter_down, "tok", axis=0, tiled=True)
    piece_count = weights_piece.shape[0]
    slot_block = slot_rows
    slot_block = slot_block.reshape(piece_count, capacity, d_local)
    partial_piece = jnp.einsum(
        "acn,arn->rac", slot_block, weights_piece, preferred_element_type=jnp.float32
    )
    partial_piece = partial_piece.reshape(low_rank, piece_count * capacity)
    low_rows = lax.psum(partial_piece, "hid").astype(jnp.bfloat16)
    weights_piece = lax.all_gather(adapter_up, "tok", axis=0, tiled=True)
    piece_count = weights_piece.shape[0]
    low_block = low_rows
    low_block = low_block.reshape(low_rank, piece_count, capacity)
    expanded = jnp.einsum(
        "rac,ark->ack", low_block, weights_piece, preferred_element_type=jnp.float32
    )
    delta_slots = expanded.astype(jnp.bfloat16).reshape(piece_count * capacity, kv_local)
    delta_rows = delta_slots[slot_index]
    return (base_sums.T + delta_rows.astype(jnp.float32)).astype(jnp.bfloat16)


def solution(mesh):
    in_specs = (
        P(("parts", "tok"), "hid"),
        P(("parts", "tok"), None),
        P("hid", None),
        P("tok", None, "hid"),
        P("tok", None, "hid"),
    )
    out_specs = P(("parts", "tok"), "hid")
    return jax.shard_map(
        per_device, mesh=mesh, in_specs=in_specs, out_specs=out_specs, check_vma=False
    )
```

profile of v0, /device:TPU:0, one launch (start us, length us, event | category | flops | bytes accessed | tf_op | source)
XLA Modules:
  0.0 95.5 jit_solution(1115968050295311452)
XLA Ops:
  7.4 0.0 all-gather.2.cloned.1.call-start
  7.4 0.7 all-gather.2.cloned.1.call-update
  8.1 0.0 reduce-scatter.2.cloned.1.call-start
  8.1 8.3 %fusion.6 = f32[1024,768]{1,0:T(8,128)} fusion(bf16[2048,1024]{1,0:T(8,128)(2,1)} %param.7, bf16[768,2048]{1,0:T(8,128)(2,1)} %param.5), kind=kOutput, calls=%fused_computation.15 | convolution fusion | flops 3221225472 | bytes 10485760 | tf_op jit(solution)/shard_map/dot_general | solution.py:26
  16.4 0.0 copy-start.1
  16.4 0.0 reduce-scatter.2.cloned.1.call-update
  16.5 0.7 copy-done.1
  17.1 0.4 convert_reduce_fusion
  17.5 0.0 copy-start
  17.5 13.4 %scatter_custom_fusion = bf16[2304,2048]{1,0:T(8,128)(2,1)} fusion(s32[768]{0:T(1024)S(1)} %fusion.5, bf16[768,2048]{1,0:T(8,128)(2,1)} %param.5, bf16[]{:T(256)} %constant.4.clone.1), kind=kCustom, calls=%fused_computation.2 | custom fusion | bytes 9437696 | tf_op jit(solution)/shard_map/scatter | solution.py:23
  30.9 0.0 copy-done
  30.9 18.3 %all_gather.7 = bf16[32,16,256]{2,1,0:T(8,128)(2,1)S(1)} all-gather(bf16[8,16,256]{2,1,0:T(8,128)(2,1)S(1)} %copy-done), channel_id=1, replica_groups=mesh['parts'=2,'tok'=4,'hid'=4] {'tok'}, dimensions={0}, use_global_device_ids=true | all-gather | bytes 327680 | tf_op jit(solution)/shard_map/all_gather | solution.py:42
  49.2 13.1 %all-gather.2.cloned.1.call-done = bf16[32,16,2048]{2,1,0:T(8,128)(2,1)} async-done(((bf16[8,16,2048]{2,1,0:T(8,128)(2,1)}), bf16[32,16,2048]{2,1,0:T(8,128)(2,1)}) %all-gather.2.cloned.1.call-update) | async-done | bytes 2097168 | tf_op jit(solution)/shard_map/all_gather | solution.py:33
  62.4 6.8 %convolution_bitcast_fusion = f32[16,32,72]{2,0,1:T(8,128)S(1)} fusion(bf16[32,72,2048]{2,1,0:T(8,128)(2,1)} %bitcast.13, bf16[32,16,2048]{2,1,0:T(8,128)(2,1)} %all-gather.2.cloned.1.call-done), kind=kOutput, calls=%fused_computation.8 | convolution fusion | flops 150994944 | bytes 11681792 | tf_op jit(solution)/shard_map/acn,arn->rac/dot_general | solution.py:37
  69.2 0.1 copy.16
  69.3 0.2 reshape.15
  69.5 12.8 %all-reduce.1 = bf16[16,2304]{1,0:T(8,128)(2,1)S(1)} all-reduce(f32[16,2304]{1,0:T(8,128)S(1)} %reshape.15), channel_id=1, replica_groups=mesh['parts'=2,'tok'=4,'hid'=4] {'hid'}, use_global_device_ids=true, to_apply=%region_3.0 | all-reduce | flops 36864 | bytes 221184 | tf_op jit(solution)/shard_map/psum | solution.py:41
  82.3 0.3 reshape.16
  82.6 0.5 convolution_convert_fusion
  83.1 2.7 %gather_fusion = bf16[768,256]{1,0:T(8,128)(2,1)S(1)} fusion(bf16[2304,256]{1,0:T(8,128)(2,1)S(1)} %bitcast.14, s32[1024]{0:T(1024)S(1)} %pad_clamp_fusion), kind=kCustom, calls=%fused_computation | custom fusion | bytes 789504 | tf_op jit(solution)/shard_map/gather | solution.py:50
  85.7 0.2 copy.18
  85.9 0.0 reduce-scatter.2.cloned.1.call-done
  85.9 1.2 %fusion.3 = bf16[768,256]{0,1:T(8,128)(2,1)S(1)} fusion(f32[256,768]{1,0:T(8,128)} %reduce-scatter.2.cloned.1.call-done, bf16[768,256]{0,1:T(8,128)(2,1)S(1)} %copy.18), kind=kLoop, calls=%fused_computation.10 | loop fusion | flops 589824 | bytes 1572864 | tf_op jit(solution)/shard_map/convert_element_type | solution.py:51
  87.1 0.9 copy.19
  (3 shorter events, 0.0 us)
Async XLA Ops:
  7.4 55.0 %all-gather.2.cloned.1.call-start = ((), (), s32[]{:S(2)}) async-start(), calls=%async_computation.2 | async-start | bytes 2621440 | tf_op jit(solution)/shard_map/all_gather | solution.py:33
  8.1 77.8 %reduce-scatter.2.cloned.1.call-start = ((), (), s32[]{:S(2)}) async-start(), calls=%async_computation.1 | async-start | bytes 3932160 | tf_op jit(solution)/shard_map/reduce_scatter | solution.py:25
  16.4 0.7 copy-start.1
  17.5 13.4 %copy-start = (bf16[8,16,256]{2,1,0:T(8,128)(2,1)S(1)}, bf16[8,16,256]{2,1,0:T(8,128)(2,1)}, u32[]{:S(2)}) copy-start(bf16[8,16,256]{2,1,0:T(8,128)(2,1)} %param.9) | copy-start | bytes 196612
Sparse Core Ops, SparseCore 0:
  9.7 52.5 all-gather.1
Sparse Core Ops, SparseCore 1:
  16.5 40.4 reduce-scatter.1
where the time goes:
time: 95.7 us; the launch traced here: 95.5 us
  blocking collectives  31.1 us (32%)
  local copies, waits for them, and re-layouts  18.4 us (19%)
  matrix products  15.6 us (16%)
  between operations  14.9 us (16%)
  waiting for transfers between devices  13.9 us (15%)
  other arithmetic  1.6 us (2%)
    all_gather x1, blocking collectives, per_device(): weights_piece = lax.all_gather(adapter_up, 'tok', axis=0, tiled=True)  18.3 us
    scatter x1, local copies, waits for them, and re-layouts, per_device(): jnp.zeros((adapters_all * capacity, d_local), jnp.bfloat16).at[slot_index]  13.4 us
    all_gather x1, waiting for transfers between devices, per_device(): weights_piece = lax.all_gather(adapter_down, 'tok', axis=0, tiled=True)  13.1 us
    psum x1, blocking collectives, per_device(): low_rows = lax.psum(partial_piece, 'hid').astype(jnp.bfloat16)  12.8 us
    dot_general x1, matrix products, per_device(): lax.dot_general(value_weight, tokens, (((0,), (1,)), ((), ())), preferred...  8.29 us
    dot_general x1, matrix products, per_device(): jnp.einsum('acn,arn->rac', slot_block, weights_piece, preferred_element_t...  6.83 us
    gather x2, local copies, waits for them, and re-layouts, per_device(): delta_rows = delta_slots[slot_index]  2.83 us
  transfers between devices with their start and end apart: 2, of which 1 were waited for; matrix products, arithmetic and copies ran while one was open for 34% of the time, Pallas kernels for 0%

commit v1 on v0

--- a/solution.py
+++ b/solution.py
@@ -38,7 +38,7 @@
         "acn,arn->rac", slot_block, weights_piece, preferred_element_type=jnp.float32
     )
     partial_piece = partial_piece.reshape(low_rank, piece_count * capacity)
-    low_rows = lax.psum(partial_piece, "hid").astype(jnp.bfloat16)
+    low_rows = jnp.sum(lax.all_gather(partial_piece, "hid"), axis=0).astype(jnp.bfloat16)
     weights_piece = lax.all_gather(adapter_up, "tok", axis=0, tiled=True)
     piece_count = weights_piece.shape[0]
     low_block = low_rows

time: 95.7 us -> 90.4 us (0.945)
  blocking collectives: 31.1 us -> 25.8 us
    psum x1 -> x0, blocking collectives: 12.8 us -> none  [per_device(): low_rows = lax.psum(partial_piece, 'hid').astype(jnp.bfloat16)]
    all_gather x0 -> x1, blocking collectives: none -> 7.51 us  [per_device(): lax.all_gather(partial_piece, 'hid')]
  transfers between devices with their start and end apart: 2 -> 2, of which waited for: 1 -> 1; matrix products, arithmetic and copies ran while one was open for 34% -> 36% of each run, Pallas kernels for 0% -> 0%
where the time goes in v1:
time: 90.4 us; the launch traced here: 90.2 us
  blocking collectives  25.8 us (29%)
  local copies, waits for them, and re-layouts  18.4 us (20%)
  matrix products  15.6 us (17%)
  between operations  14.9 us (16%)
  waiting for transfers between devices  13.9 us (15%)
  other arithmetic  1.63 us (2%)
    all_gather x1, blocking collectives, per_device(): weights_piece = lax.all_gather(adapter_up, 'tok', axis=0, tiled=True)  18.3 us
    scatter x1, local copies, waits for them, and re-layouts, per_device(): jnp.zeros((adapters_all * capacity, d_local), jnp.bfloat16).at[slot_index]  13.4 us
    all_gather x1, waiting for transfers between devices, per_device(): weights_piece = lax.all_gather(adapter_down, 'tok', axis=0, tiled=True)  13.1 us
    dot_general x1, matrix products, per_device(): lax.dot_general(value_weight, tokens, (((0,), (1,)), ((), ())), preferred...  8.29 us
    all_gather x1, blocking collectives, per_device(): lax.all_gather(partial_piece, 'hid')  7.51 us
    dot_general x1, matrix products, per_device(): jnp.einsum('acn,arn->rac', slot_block, weights_piece, preferred_element_t...  6.83 us
    gather x2, local copies, waits for them, and re-layouts, per_device(): delta_rows = delta_slots[slot_index]  2.83 us
  transfers between devices with their start and end apart: 2, of which 1 were waited for; matrix products, arithmetic and copies ran while one was open for 36% of the time, Pallas kernels for 0%

profile of v1, /device:TPU:0, one launch (start us, length us, event | category | flops | bytes accessed | tf_op | source)
XLA Modules:
  0.0 90.2 jit_solution(12641079637155354506)
XLA Ops:
  7.4 0.0 all-gather.2.cloned.1.call-start
  7.4 0.7 all-gather.2.cloned.1.call-update
  8.1 0.0 reduce-scatter.2.cloned.1.call-start
  8.1 8.3 %fusion.6 = f32[1024,768]{1,0:T(8,128)} fusion(bf16[2048,1024]{1,0:T(8,128)(2,1)} %param.7, bf16[768,2048]{1,0:T(8,128)(2,1)} %param.5), kind=kOutput, calls=%fused_computation.15 | convolution fusion | flops 3221225472 | bytes 10485760 | tf_op jit(solution)/shard_map/dot_general | solution.py:26
  16.4 0.0 copy-start.1
  16.4 0.0 reduce-scatter.2.cloned.1.call-update
  16.5 0.7 copy-done.1
  17.1 0.4 convert_reduce_fusion
  17.5 0.0 copy-start
  17.5 13.4 %scatter_custom_fusion = bf16[2304,2048]{1,0:T(8,128)(2,1)} fusion(s32[768]{0:T(1024)S(1)} %fusion.5, bf16[768,2048]{1,0:T(8,128)(2,1)} %param.5, bf16[]{:T(256)} %constant.5.clone.1), kind=kCustom, calls=%fused_computation.2 | custom fusion | bytes 9437696 | tf_op jit(solution)/shard_map/scatter | solution.py:23
  30.9 0.0 copy-done
  30.9 18.3 %all_gather.11 = bf16[32,16,256]{2,1,0:T(8,128)(2,1)S(1)} all-gather(bf16[8,16,256]{2,1,0:T(8,128)(2,1)S(1)} %copy-done), channel_id=1, replica_groups=mesh['parts'=2,'tok'=4,'hid'=4] {'tok'}, dimensions={0}, use_global_device_ids=true | all-gather | bytes 327680 | tf_op jit(solution)/shard_map/all_gather | solution.py:42
  49.2 13.1 %all-gather.2.cloned.1.call-done = bf16[32,16,2048]{2,1,0:T(8,128)(2,1)} async-done(((bf16[8,16,2048]{2,1,0:T(8,128)(2,1)}), bf16[32,16,2048]{2,1,0:T(8,128)(2,1)}) %all-gather.2.cloned.1.call-update) | async-done | bytes 2097168 | tf_op jit(solution)/shard_map/all_gather | solution.py:33
  62.4 6.8 %convolution_bitcast_fusion = f32[16,32,72]{2,0,1:T(8,128)S(1)} fusion(bf16[32,72,2048]{2,1,0:T(8,128)(2,1)} %bitcast.13, bf16[32,16,2048]{2,1,0:T(8,128)(2,1)} %all-gather.2.cloned.1.call-done), kind=kOutput, calls=%fused_computation.8 | convolution fusion | flops 150994944 | bytes 11681792 | tf_op jit(solution)/shard_map/acn,arn->rac/dot_general | solution.py:37
  69.2 0.1 copy.16
  69.3 0.2 all_gather_reshape.3
  69.5 7.5 %all_gather.10 = f32[4,16,2304]{2,1,0:T(8,128)S(1)} all-gather(f32[1,16,2304]{2,1,0:T(8,128)S(1)} %all_gather_reshape.3), channel_id=1, replica_groups=mesh['parts'=2,'tok'=4,'hid'=4] {'hid'}, dimensions={0}, use_global_device_ids=true | all-gather | bytes 737280 | tf_op jit(solution)/shard_map/all_gather | solution.py:41
  77.0 0.3 convert_element_type.21
  77.3 0.5 convolution_convert_fusion
  77.8 2.7 %gather_fusion = bf16[768,256]{1,0:T(8,128)(2,1)S(1)} fusion(bf16[2304,256]{1,0:T(8,128)(2,1)S(1)} %bitcast.14, s32[1024]{0:T(1024)S(1)} %pad_clamp_fusion), kind=kCustom, calls=%fused_computation | custom fusion | bytes 789504 | tf_op jit(solution)/shard_map/gather | solution.py:50
  80.4 0.2 copy.18
  80.6 0.0 reduce-scatter.2.cloned.1.call-done
  80.7 1.2 %fusion.3 = bf16[768,256]{0,1:T(8,128)(2,1)S(1)} fusion(f32[256,768]{1,0:T(8,128)} %reduce-scatter.2.cloned.1.call-done, bf16[768,256]{0,1:T(8,128)(2,1)S(1)} %copy.18), kind=kLoop, calls=%fused_computation.10 | loop fusion | flops 589824 | bytes 1572864 | tf_op jit(solution)/shard_map/convert_element_type | solution.py:51
  81.9 0.9 %copy.19 = bf16[768,256]{1,0:T(8,128)(2,1)} copy(bf16[768,256]{0,1:T(8,128)(2,1)S(1)} %fusion.3) | data formatting | bytes 786432 | tf_op jit(solution)/shard_map/convert_element_type | solution.py:51
  (4 shorter events, 0.1 us)
Async XLA Ops:
  7.4 55.0 %all-gather.2.cloned.1.call-start = ((), (), s32[]{:S(2)}) async-start(), calls=%async_computation.2 | async-start | bytes 2621440 | tf_op jit(solution)/shard_map/all_gather | solution.py:33
  8.1 72.6 %reduce-scatter.2.cloned.1.call-start = ((), (), s32[]{:S(2)}) async-start(), calls=%async_computation.1 | async-start | bytes 3932160 | tf_op jit(solution)/shard_map/reduce_scatter | solution.py:25
  16.4 0.7 copy-start.1
  17.5 13.4 %copy-start = (bf16[8,16,256]{2,1,0:T(8,128)(2,1)S(1)}, bf16[8,16,256]{2,1,0:T(8,128)(2,1)}, u32[]{:S(2)}) copy-start(bf16[8,16,256]{2,1,0:T(8,128)(2,1)} %param.9) | copy-start | bytes 196612
Sparse Core Ops, SparseCore 0:
  9.7 52.5 all-gather.1
Sparse Core Ops, SparseCore 1:
  16.5 40.4 reduce-scatter.1
